TPU v7x, 32 devices: a whole 2x2x4 slice. The times are simulated.
32 devices in a mesh: dp: 8 (over y, x, core), expert: 4 (over z).
Axes of the slice: x: 2, y: 2, z: 4, core: 2. Of those that a mesh axis runs over, the one named last changes fastest.
Arguments:
- policy_hidden: bfloat16 [1024, 4096], P('dp', 'expert'), may hold values from -6 to 6
- reference_hidden: bfloat16 [1024, 4096], P('dp', 'expert'), may hold values from -6 to 6
- policy_norm_gain: float32 [4096], P('expert'), may hold values from 0.25 to 1.75
- reference_norm_gain: float32 [4096], P('expert'), may hold values from 0.25 to 1.75
- policy_router: float32 [4096, 4], P('expert'), may hold values from -5.1875 to 5.1875
- reference_router: float32 [4096, 4], P('expert'), may hold values from -5.1875 to 5.1875
- policy_gate: bfloat16 [4, 4096, 8192], P('expert', 'dp'), may hold values from -0.09375 to 0.09375
- policy_up: bfloat16 [4, 4096, 8192], P('expert', 'dp'), may hold values from -0.09375 to 0.09375
- policy_down: bfloat16 [4, 8192, 4096], P('expert', 'dp'), may hold values from -0.0625 to 0.0625
- reference_gate: bfloat16 [4, 4096, 8192], P('expert', 'dp'), may hold values from -0.09375 to 0.09375
- reference_up: bfloat16 [4, 4096, 8192], P('expert', 'dp'), may hold values from -0.09375 to 0.09375
- reference_down: bfloat16 [4, 8192, 4096], P('expert', 'dp'), may hold values from -0.0625 to 0.0625
- expert_ids: int32 [1024, 2], P('dp'), may hold values from 0 to 3, all different within a row; in each aligned block of 128 rows (0 to 127, 128 to 255, ...) at most 96 rows name the same one
- lengths: int32 [32], P('dp'), may hold values from 1 to 32, as said below
Outputs:
- policy_mixture: bfloat16 [1024, 4096], P('dp', 'expert')
- reference_mixture: bfloat16 [1024, 4096], P('dp', 'expert')
- token_kl: float32 [1024], P('dp')
- loss: float32 [], replicated
Inputs may be any that keep to these rules, and one draw needn't show every extreme that they name: `expert_ids`: each row names 2 different experts; among the rows of one index of dp (aligned blocks of 128 rows) no expert is named more than 96 times, and in some block one expert is named exactly 96 times. The first lengths[r] of rollout r's 32 positions are live.
All inputs are finite; a program needn't handle non-finite values.
Results may differ from a plain program's by a relative error of at most 0.02.
Values may be sent and summed in bfloat16 or wider, within the bound.
A program may use at most 256 MiB of HBM per device.

v0:
```python
import jax
import jax.numpy as jnp
from jax import lax
from jax.sharding import PartitionSpec as P

D = 4096
SEG = 32


EPSILON = 1e-05
KL_WEIGHT = 1.0
BALANCE_WEIGHT = 0.5


def router_terms(hidden, norm_gain, router):
    values = hidden.astype(jnp.float32)
    partial_logits = jnp.dot(values * norm_gain, router, precision=lax.Precision.HIGHEST)
    return (partial_logits, jnp.sum(values * values, axis=1))


def expert_terms(piece_rows, weights):
    results = []
    for model_index in range(len(weights)):
        gate_weight, up_weight, down_weight = weights[model_index]
        model_rows = piece_rows[:, model_index, :]
        gate_value = jnp.dot(model_rows, gate_weight, preferred_element_type=jnp.float32)
        up_value = jnp.dot(model_rows, up_weight, preferred_element_type=jnp.float32)
        hidden = (jax.nn.silu(gate_value) * up_value).astype(jnp.bfloat16)
        results.append(jnp.dot(hidden, down_weight, preferred_element_type=jnp.float32))
    return jnp.stack(results, axis=1)


def mixture(slot_rows, weights):
    expert_count, slot_count, models, feature_block = slot_rows.shape
    model_width = expert_count * feature_block
    arrived_rows = lax.all_to_all(slot_rows, "expert", split_axis=0, concat_axis=3, tiled=True)
    local_rows = arrived_rows.reshape(slot_count, models, model_width)
    partial_terms = expert_terms(
        lax.all_gather(local_rows, "dp", axis=0, tiled=True), weights
    ).astype(jnp.bfloat16)
    summed = (
        lax.psum_scatter(partial_terms, "dp", scatter_dimension=0, tiled=True)
        .astype(jnp.float32)
        .astype(jnp.bfloat16)
    )
    result = lax.all_to_all(
        summed.reshape(1, slot_count, models, model_width),
        "expert",
        split_axis=3,
        concat_axis=0,
        tiled=True,
    )
    return result


def per_device(
    policy_hidden,
    reference_hidden,
    policy_norm_gain,
    reference_norm_gain,
    policy_router,
    reference_router,
    policy_gate,
    policy_up,
    policy_down,
    reference_gate,
    reference_up,
    reference_down,
    expert_ids,
    lengths,
):
    expert_count = lax.axis_size("expert")
    token_count, feature_block = policy_hidden.shape
    route_count = expert_ids.shape[1]
    slot_count = 3 * token_count // expert_count
    token_total = float(token_count * lax.axis_size("dp"))
    policy_partial, policy_squares = router_terms(policy_hidden, policy_norm_gain, policy_router)
    reference_partial, reference_squares = router_terms(
        reference_hidden, reference_norm_gain, reference_router
    )
    policy_partial, reference_partial, policy_squares, reference_squares = lax.psum(
        (policy_partial, reference_partial, policy_squares, reference_squares), "expert"
    )
    policy_scale = lax.rsqrt(policy_squares / D + EPSILON)[:, None]
    reference_scale = lax.rsqrt(reference_squares / D + EPSILON)[:, None]
    policy_logits = policy_partial * policy_scale
    reference_logits = reference_partial * reference_scale
    policy_rows = (policy_hidden.astype(jnp.float32) * policy_norm_gain * policy_scale).astype(
        jnp.bfloat16
    )
    reference_rows = (
        reference_hidden.astype(jnp.float32) * reference_norm_gain * reference_scale
    ).astype(jnp.bfloat16)
    live_mask = (
        (jnp.arange(SEG, dtype=jnp.int32)[None, :] < lengths[:, None])
        .reshape(-1)
        .astype(jnp.float32)
    )
    flat_ids = expert_ids.reshape(-1)
    onehot = (flat_ids[:, None] == jnp.arange(expert_count, dtype=jnp.int32)[None, :]).astype(
        jnp.int32
    )
    before = jnp.cumsum(onehot, axis=0) - onehot
    target = flat_ids * slot_count + jnp.sum(before * onehot, axis=1)
    slot_index = jnp.arange(expert_count * slot_count, dtype=jnp.int32)
    select = jnp.any(
        slot_index[:, None, None] == target.reshape(token_count, route_count)[None, :, :], axis=2
    ).astype(jnp.bfloat16)

    def pair_gates(logits):
        matches = expert_ids[:, :, None] == jnp.arange(expert_count, dtype=jnp.int32)[None, None, :]
        chosen = jnp.sum(jnp.where(matches, logits[:, None, :], 0.0), axis=2)
        return jax.nn.softmax(chosen, axis=1)

    def combine(expert_output, gates):
        picked = jnp.take(
            expert_output.reshape(expert_count * slot_count, feature_block), target, axis=0
        )
        picked = picked.reshape(token_count, route_count, feature_block).astype(jnp.float32)
        mixed_rows = jnp.sum(picked * gates[:, :, None], axis=1) * live_mask[:, None]
        return mixed_rows.astype(jnp.bfloat16)

    policy_gate_full, policy_up_full, reference_gate_full, reference_up_full = (
        lax.all_to_all(policy_gate, "dp", split_axis=2, concat_axis=1, tiled=True),
        lax.all_to_all(policy_up, "dp", split_axis=2, concat_axis=1, tiled=True),
        lax.all_to_all(reference_gate, "dp", split_axis=2, concat_axis=1, tiled=True),
        lax.all_to_all(reference_up, "dp", split_axis=2, concat_axis=1, tiled=True),
    )
    stacked_rows = jnp.concatenate((policy_rows, reference_rows), axis=1)
    placed = jnp.dot(select, stacked_rows, preferred_element_type=jnp.float32).astype(jnp.bfloat16)
    expert_output = mixture(
        placed.reshape(expert_count, slot_count, 2, feature_block),
        (
            (policy_gate_full[0], policy_up_full[0], policy_down[0]),
            (reference_gate_full[0], reference_up_full[0], reference_down[0]),
        ),
    )
    policy_output = expert_output[:, :, 0, :]
    reference_output = expert_output[:, :, 1, :]
    policy_mixture = combine(policy_output, pair_gates(policy_logits))
    reference_mixture = combine(reference_output, pair_gates(reference_logits))
    policy_logprob = jax.nn.log_softmax(policy_logits, axis=1)
    reference_logprob = jax.nn.log_softmax(reference_logits, axis=1)
    policy_prob = jnp.exp(policy_logprob)
    token_kl = jnp.sum(policy_prob * (policy_logprob - reference_logprob), axis=1) * live_mask
    route_onehot = onehot.reshape(token_count, route_count, expert_count)
    counts = jnp.sum(jnp.sum(route_onehot, axis=1).astype(jnp.float32) * live_mask[:, None], axis=0)
    probsum = jnp.sum(policy_prob * live_mask[:, None], axis=0)
    counts, probsum, kl_total = lax.psum((counts, probsum, jnp.sum(token_kl)), "dp")
    balance = expert_count * jnp.sum(counts / (route_count * token_total) * probsum / token_total)
    loss = KL_WEIGHT * kl_total / token_total + BALANCE_WEIGHT * balance
    return (policy_mixture, reference_mixture, token_kl, loss)


def solution(mesh):
    in_specs = (
        P("dp", "expert"),
        P("dp", "expert"),
        P("expert"),
        P("expert"),
        P("expert", None),
        P("expert", None),
        P("expert", "dp", None),
        P("expert", "dp", None),
        P("expert", "dp", None),
        P("expert", "dp", None),
        P("expert", "dp", None),
        P("expert", "dp", None),
        P("dp", None),
        P("dp"),
    )
    out_specs = (P("dp", "expert"), P("dp", "expert"), P("dp"), P())
    return jax.shard_map(
        per_device, mesh=mesh, in_specs=in_specs, out_specs=out_specs, check_vma=False
    )
```

profile of v0, /device:TPU:0, one launch (start us, length us, event | category | flops | bytes accessed | tf_op | source)
XLA Modules:
  0.0 886.3 jit_solution(8897518437984197567)
XLA Ops:
  11.9 1.5 fusion.22
  13.4 14.3 %all-reduce.1 = (f32[128]{0:T(128)S(1)}, f32[128]{0:T(128)S(1)}, f32[128,4]{0,1:T(4,128)}, f32[128,4]{0,1:T(4,128)}) all-reduce(f32[128]{0:T(128)S(1)} %fusion.27, f32[128]{0:T(128)S(1)} %fusion.26, f32[128,4]{0,1:T(4,128)S(1)} %fusion.22, f32[128,4]{0,1:T(4,128)S(1)} %fusion.20), channel_id=1, replica_groups=mesh['dp'=8,'expert'=4] {'expert'}, use_global_device_ids=true, to_apply=%region_7.8 | all-reduce | flops 1280 | bytes 10240 | tf_op jit(solution)/shard_map/psum | solution.py:81
  34.2 1.7 copy.105
  35.9 3.6 all-to-all-start
  39.5 34.5 %copy.109 = bf16[1,512,8192]{1,0,2:T(2,128)(2,1)} copy(bf16[1,512,8192]{2,1,0:T(8,128)(2,1)} %param.24) | data formatting | bytes 16777216 | tf_op args[7]
  74.5 54.6 %reduce.6 = bf16[8192,512]{1,0:T(8,128)(2,1)} reduce(bf16[8192,1,512]{2,1,0:T(2,128)(2,1)} %bitcast.98, bf16[]{:T(256)} %broadcast.143), dimensions={1}, to_apply=%bitcast.81.reduce_sub_computation | reduce | bytes 16777218
  129.1 11.2 %reshape.201 = bf16[8,2,262144]{2,1,0:T(2,128)(2,1)} reshape(bf16[8192,512]{1,0:T(8,128)(2,1)} %reduce.6) | data formatting | bytes 16777216
  140.2 5.2 all-to-all-start.2
  145.4 34.5 %copy.107 = bf16[1,512,8192]{1,0,2:T(2,128)(2,1)} copy(bf16[1,512,8192]{2,1,0:T(8,128)(2,1)} %param.23) | data formatting | bytes 16777216 | tf_op args[6]
  180.0 54.6 %reduce.7 = bf16[8192,512]{1,0:T(8,128)(2,1)} reduce(bf16[8192,1,512]{2,1,0:T(2,128)(2,1)} %bitcast.100, bf16[]{:T(256)} %broadcast.143), dimensions={1}, to_apply=%bitcast.83.reduce_sub_computation | reduce | bytes 16777218
  234.6 11.2 %reshape.203 = bf16[8,2,262144]{2,1,0:T(2,128)(2,1)} reshape(bf16[8192,512]{1,0:T(8,128)(2,1)} %reduce.7) | data formatting | bytes 16777216
  245.8 4.9 all-to-all-start.1
  252.0 2.4 reshape.171
  254.4 34.7 %copy.113 = bf16[1,512,8192]{1,0,2:T(2,128)(2,1)} copy(bf16[1,512,8192]{2,1,0:T(8,128)(2,1)} %param.27) | data formatting | bytes 16777216 | tf_op args[10]
  289.2 54.6 %reduce.4 = bf16[8192,512]{1,0:T(8,128)(2,1)} reduce(bf16[8192,1,512]{2,1,0:T(2,128)(2,1)} %bitcast.101, bf16[]{:T(256)} %broadcast.143), dimensions={1}, to_apply=%bitcast.77.reduce_sub_computation | reduce | bytes 16777218
  343.7 11.2 %reshape.197 = bf16[8,2,262144]{2,1,0:T(2,128)(2,1)} reshape(bf16[8192,512]{1,0:T(8,128)(2,1)} %reduce.4) | data formatting | bytes 16777216
  354.9 36.7 %all-to-all-done.1 = bf16[8,2,262144]{2,1,0:T(2,128)(2,1)} async-done(((bf16[8,2,262144]{2,1,0:T(2,128)(2,1)}), bf16[8,2,262144]{2,1,0:T(2,128)(2,1)}, u32[]{:S(2)}, u32[]{:S(2)}) %all-to-all-start.1) | async-done | bytes 8388640 | tf_op jit(solution)/shard_map/all_to_all | solution.py:124
  391.6 5.4 all-to-all-start.4
  397.0 34.5 %copy.111 = bf16[1,512,8192]{1,0,2:T(2,128)(2,1)} copy(bf16[1,512,8192]{2,1,0:T(8,128)(2,1)} %param.26) | data formatting | bytes 16777216 | tf_op args[9]
  431.5 54.6 %reduce.5 = bf16[8192,512]{1,0:T(8,128)(2,1)} reduce(bf16[8192,1,512]{2,1,0:T(2,128)(2,1)} %bitcast.99, bf16[]{:T(256)} %broadcast.143), dimensions={1}, to_apply=%bitcast.79.reduce_sub_computation | reduce | bytes 16777218
  486.1 11.2 %reshape.199 = bf16[8,2,262144]{2,1,0:T(2,128)(2,1)} reshape(bf16[8192,512]{1,0:T(8,128)(2,1)} %reduce.5) | data formatting | bytes 16777216
  497.3 4.9 all-to-all-start.3
  502.3 13.3 %reshape.202 = bf16[8192,1,512]{2,1,0:T(2,128)(2,1)} reshape(bf16[8,2,262144]{2,1,0:T(2,128)(2,1)} %all-to-all-done.2) | data formatting | bytes 16777216
  515.6 11.6 %copy.120 = bf16[1,512,8192]{1,2,0:T(8,128)(2,1)} copy(bf16[1,512,8192]{1,0,2:T(2,128)(2,1)} %bitcast.94) | data formatting | bytes 16777216
  527.2 11.4 %copy.110 = bf16[1,8,512,1024]{3,2,1,0:T(8,128)(2,1)} copy(bf16[1,8,512,1024]{2,3,1,0:T(8,128)(2,1)} %bitcast.102) | data formatting | bytes 16777216 | tf_op jit(solution)/shard_map/all_to_all | solution.py:125
  538.7 13.3 %reshape.204 = bf16[8192,1,512]{2,1,0:T(2,128)(2,1)} reshape(bf16[8,2,262144]{2,1,0:T(2,128)(2,1)} %all-to-all-done.1) | data formatting | bytes 16777216
  552.0 11.6 %copy.119 = bf16[1,512,8192]{1,2,0:T(8,128)(2,1)} copy(bf16[1,512,8192]{1,0,2:T(2,128)(2,1)} %bitcast.95) | data formatting | bytes 16777216
  563.6 11.4 %copy.108 = bf16[1,8,512,1024]{3,2,1,0:T(8,128)(2,1)} copy(bf16[1,8,512,1024]{2,3,1,0:T(8,128)(2,1)} %bitcast.103) | data formatting | bytes 16777216 | tf_op jit(solution)/shard_map/all_to_all | solution.py:124
  575.0 13.3 %reshape.198 = bf16[8192,1,512]{2,1,0:T(2,128)(2,1)} reshape(bf16[8,2,262144]{2,1,0:T(2,128)(2,1)} %all-to-all-done.4) | data formatting | bytes 16777216
  588.3 11.6 %copy.122 = bf16[1,512,8192]{1,2,0:T(8,128)(2,1)} copy(bf16[1,512,8192]{1,0,2:T(2,128)(2,1)} %bitcast.96) | data formatting | bytes 16777216
  600.0 11.5 %copy.114 = bf16[1,8,512,1024]{3,2,1,0:T(8,128)(2,1)} copy(bf16[1,8,512,1024]{2,3,1,0:T(8,128)(2,1)} %bitcast.104) | data formatting | bytes 16777216 | tf_op jit(solution)/shard_map/all_to_all | solution.py:127
  611.4 13.3 %reshape.200 = bf16[8192,1,512]{2,1,0:T(2,128)(2,1)} reshape(bf16[8,2,262144]{2,1,0:T(2,128)(2,1)} %all-to-all-done.3) | data formatting | bytes 16777216
  624.7 11.8 %copy.121 = bf16[1,512,8192]{1,2,0:T(8,128)(2,1)} copy(bf16[1,512,8192]{1,0,2:T(2,128)(2,1)} %bitcast.97) | data formatting | bytes 16777216
  636.6 11.5 %copy.112 = bf16[1,8,512,1024]{3,2,1,0:T(8,128)(2,1)} copy(bf16[1,8,512,1024]{2,3,1,0:T(8,128)(2,1)} %bitcast.105) | data formatting | bytes 16777216 | tf_op jit(solution)/shard_map/all_to_all | solution.py:126
  648.0 11.0 %fusion.16 = f32[768,1024]{1,0:T(8,128)S(1)} fusion(bf16[4096,1024]{1,0:T(8,128)(2,1)} %bitcast.109, bf16[768,2,4096]{2,0,1:T(8,128)(2,1)} %all-gather.2.cloned.1.call-done), kind=kOutput, calls=%fused_computation.13 | convolution fusion | flops 6442450944 | bytes 17825792 | tf_op jit(solution)/shard_map/dot_general | solution.py:27
  659.1 9.7 %multiply_convert_fusion.1 = bf16[768,1024]{1,0:T(8,128)(2,1)S(1)} fusion(f32[768,1024]{1,0:T(8,128)S(1)} %fusion.16, bf16[4096,1024]{1,0:T(8,128)(2,1)} %bitcast.110, bf16[768,2,4096]{2,0,1:T(8,128)(2,1)S(1)} %copy-done.13), kind=kOutput, calls=%fused_computation.18 | convolution fusion | flops 6447169536 | bytes 19398656 | tf_op jit(solution)/shard_map/dot_general | solution.py:26
  668.8 10.6 %fusion.13 = bf16[768,1,4096]{2,0,1:T(8,128)(2,1)S(1)} fusion(bf16[768,1024]{1,0:T(8,128)(2,1)S(1)} %multiply_convert_fusion.1, bf16[1,1024,4096]{2,1,0:T(8,128)(2,1)} %param.25), kind=kOutput, calls=%fused_computation.12 | convolution fusion | flops 6445596672 | bytes 16252928 | tf_op jit(solution)/shard_map/dot_general | solution.py:29
  679.5 10.2 %fusion.18 = f32[768,1024]{1,0:T(8,128)} fusion(bf16[4096,1024]{1,0:T(8,128)(2,1)S(1)} %bitcast.113, bf16[768,2,4096]{2,0,1:T(8,128)(2,1)} %all-gather.2.cloned.1.call-done), kind=kOutput, calls=%fused_computation.15 | convolution fusion | flops 6442450944 | bytes 17825792 | tf_op jit(solution)/shard_map/dot_general | solution.py:27
  689.7 10.0 %multiply_convert_fusion = bf16[768,1024]{1,0:T(8,128)(2,1)S(1)} fusion(f32[768,1024]{1,0:T(8,128)} %fusion.18, bf16[4096,1024]{1,0:T(8,128)(2,1)S(1)} %bitcast.116, bf16[768,2,4096]{2,0,1:T(8,128)(2,1)} %all-gather.2.cloned.1.call-done), kind=kOutput, calls=%fused_computation.17 | convolution fusion | flops 6447169536 | bytes 19398656 | tf_op jit(solution)/shard_map/dot_general | solution.py:26
  699.7 7.3 fusion.10
  707.0 5.4 pad_maximum_fusion
  712.5 94.5 %reduce-scatter.2.cloned.1.call-done = bf16[96,2,4096]{2,0,1:T(8,128)(2,1)} async-done(((bf16[768,2,4096]{2,0,1:T(8,128)(2,1)}), bf16[96,2,4096]{2,0,1:T(8,128)(2,1)}) %reduce-scatter.2.cloned.1.call-update) | async-done | bytes 1572880 | tf_op jit(solution)/shard_map/reduce_scatter | solution.py:42
  807.0 5.7 copy.115
  812.7 4.6 all-to-all-start.5
  818.9 13.4 %all-reduce = (f32[]{:T(128)}, f32[4]{0:T(128)S(1)}, f32[4]{0:T(128)S(1)}) all-reduce(f32[]{:T(128)} %get-tuple-element.18, f32[4]{0:T(128)S(1)} %get-tuple-element.6, f32[4]{0:T(128)S(1)} %get-tuple-element.10), channel_id=1, replica_groups=mesh['dp'=8,'expert'=4] {'dp'}, use_global_device_ids=true, to_apply=%region_23.26 | all-reduce | flops 9 | bytes 72 | tf_op jit(solution)/shard_map/psum | solution.py:149
  834.7 30.7 %all-to-all-done.5 = bf16[1,96,2,4096]{1,2,0,3:T(2,128)(2,1)S(1)} async-done(((bf16[1,96,2,4096]{1,2,0,3:T(2,128)(2,1)}), bf16[1,96,2,4096]{1,2,0,3:T(2,128)(2,1)S(1)}, u32[]{:S(2)}, u32[]{:S(2)}) %all-to-all-start.5) | async-done | bytes 1572896 | tf_op jit(solution)/shard_map/all_to_all | solution.py:46
  865.4 3.7 copy.116
  869.1 1.6 fusion.47
  (112 shorter events, 23.1 us)
Async XLA Ops:
  7.2 3.3 copy-start
  8.3 24.2 %copy-start.3 = (s32[256]{0:T(256)}, s32[256]{0:T(256)S(1)}, u32[]{:S(2)}) copy-start(s32[256]{0:T(256)S(1)} %eq.60) | copy-start | bytes 3076
  27.7 1.1 copy-start.9
  27.7 2.1 copy-start.7
  31.5 42.5 %copy-start.5 = (s32[256]{0:T(256)}, s32[256]{0:T(256)S(1)}, u32[]{:S(2)}) copy-start(s32[256]{0:T(256)S(1)} %fusion.36) | copy-start | bytes 3076
  35.9 104.3 %all-to-all-start = ((bf16[4,96,2,1024]{3,1,2,0:T(8,128)(2,1)}), bf16[4,96,2,1024]{3,1,2,0:T(8,128)(2,1)S(1)}, u32[]{:S(2)}, u32[]{:S(2)}) async-start(bf16[4,96,2,1024]{3,1,2,0:T(8,128)(2,1)} %copy.105), calls=%async_computation | async-start | bytes 3145728 | tf_op jit(solution)/shard_map/all_to_all | solution.py:36
  140.2 105.5 %all-to-all-start.2 = ((bf16[8,2,262144]{2,1,0:T(2,128)(2,1)}), bf16[8,2,262144]{2,1,0:T(2,128)(2,1)}, u32[]{:S(2)}, u32[]{:S(2)}) async-start(bf16[8,2,262144]{2,1,0:T(2,128)(2,1)} %reshape.201), calls=%async_computation.2 | async-start | bytes 16777216 | tf_op jit(solution)/shard_map/all_to_all | solution.py:125
  245.8 145.8 %all-to-all-start.1 = ((bf16[8,2,262144]{2,1,0:T(2,128)(2,1)}), bf16[8,2,262144]{2,1,0:T(2,128)(2,1)}, u32[]{:S(2)}, u32[]{:S(2)}) async-start(bf16[8,2,262144]{2,1,0:T(2,128)(2,1)} %reshape.203), calls=%async_computation.1 | async-start | bytes 16777216 | tf_op jit(solution)/shard_map/all_to_all | solution.py:124
  250.7 397.3 %all-gather.2.cloned.1.call-start = ((), (), s32[]{:S(2)}) async-start(), calls=%async_computation.7 | async-start | bytes 14155776 | tf_op jit(solution)/shard_map/all_gather | solution.py:39
  391.6 105.7 %all-to-all-start.4 = ((bf16[8,2,262144]{2,1,0:T(2,128)(2,1)}), bf16[8,2,262144]{2,1,0:T(2,128)(2,1)}, u32[]{:S(2)}, u32[]{:S(2)}) async-start(bf16[8,2,262144]{2,1,0:T(2,128)(2,1)} %reshape.197), calls=%async_computation.4 | async-start | bytes 16777216 | tf_op jit(solution)/shard_map/all_to_all | solution.py:127
  497.3 114.2 %all-to-all-start.3 = ((bf16[8,2,262144]{2,1,0:T(2,128)(2,1)}), bf16[8,2,262144]{2,1,0:T(2,128)(2,1)}, u32[]{:S(2)}, u32[]{:S(2)}) async-start(bf16[8,2,262144]{2,1,0:T(2,128)(2,1)} %reshape.199), calls=%async_computation.3 | async-start | bytes 16777216 | tf_op jit(solution)/shard_map/all_to_all | solution.py:126
  502.2 304.8 %reduce-scatter.2.cloned.1.call-start = ((), (), s32[]{:S(2)}) async-start(), calls=%async_computation.8 | async-start | bytes 14155776 | tf_op jit(solution)/shard_map/reduce_scatter | solution.py:42
  648.0 11.0 %copy-start.13 = (bf16[768,2,4096]{2,0,1:T(8,128)(2,1)S(1)}, bf16[768,2,4096]{2,0,1:T(8,128)(2,1)}, u32[]{:S(2)}) copy-start(bf16[768,2,4096]{2,0,1:T(8,128)(2,1)} %all-gather.2.cloned.1.call-done) | copy-start | bytes 37748740
  659.1 20.4 %slice-start = ((s8[8388608]{0:T(1024)(128)(4,1)}), s8[4194304]{0:T(1024)(128)(4,1)S(1)}, s32[]{:S(2)}) async-start(s8[8388608]{0:T(1024)(128)(4,1)} %bitcast.111), calls=%async_computation.9 | async-start | bytes 8388608
  668.8 10.7 %slice-start.1 = ((s8[8388608]{0:T(1024)(128)(4,1)}), s8[4194304]{0:T(1024)(128)(4,1)S(1)}, s32[]{:S(2)}) async-start(s8[8388608]{0:T(1024)(128)(4,1)} %bitcast.111), calls=%async_computation.10 | async-start | bytes 8388608
  668.8 20.9 %slice-start.2 = ((s8[8388608]{0:T(1024)(128)(4,1)}), s8[4194304]{0:T(1024)(128)(4,1)S(1)}, s32[]{:S(2)}) async-start(s8[8388608]{0:T(1024)(128)(4,1)} %bitcast.114), calls=%async_computation.11 | async-start | bytes 8388608
  668.8 30.9 %slice-start.4 = ((s8[8388608]{0:T(1024)(128)(4,1)}), s8[4194304]{0:T(1024)(128)(4,1)S(1)}, s32[]{:S(2)}) async-start(s8[8388608]{0:T(1024)(128)(4,1)} %bitcast.121), calls=%async_computation.13 | async-start | bytes 8388608
  679.5 10.2 %slice-start.3 = ((s8[8388608]{0:T(1024)(128)(4,1)}), s8[4194304]{0:T(1024)(128)(4,1)S(1)}, s32[]{:S(2)}) async-start(s8[8388608]{0:T(1024)(128)(4,1)} %bitcast.114), calls=%async_computation.12 | async-start | bytes 8388608
  679.5 20.2 %slice-start.5 = ((s8[8388608]{0:T(1024)(128)(4,1)}), s8[4194304]{0:T(1024)(128)(4,1)S(1)}, s32[]{:S(2)}) async-start(s8[8388608]{0:T(1024)(128)(4,1)} %bitcast.121), calls=%async_computation.14 | async-start | bytes 8388608
  712.4 104.9 %copy-start.14 = (s32[4]{0:T(128)S(1)}, s32[4]{0:T(128)}, u32[]{:S(2)}) copy-start(s32[4]{0:T(128)} %param.30) | copy-start | bytes 52
  712.4 105.1 %copy-start.10 = (f32[128]{0:T(128)S(1)}, f32[128]{0:T(128)}, u32[]{:S(2)}) copy-start(f32[128]{0:T(128)} %copy-done.9) | copy-start | bytes 1540
  712.4 105.1 %copy-start.12 = (f32[128,4]{0,1:T(4,128)S(1)}, f32[128,4]{0,1:T(4,128)}, u32[]{:S(2)}) copy-start(f32[128,4]{0,1:T(4,128)} %get-tuple-element.16) | copy-start | bytes 6148
  712.4 105.1 %copy-start.8 = (f32[128]{0:T(128)S(1)}, f32[128]{0:T(128)}, u32[]{:S(2)}) copy-start(f32[128]{0:T(128)} %copy-done.7) | copy-start | bytes 1540
  712.4 105.1 %copy-start.11 = (f32[128,4]{0,1:T(4,128)S(1)}, f32[128,4]{0,1:T(4,128)}, u32[]{:S(2)}) copy-start(f32[128,4]{0,1:T(4,128)} %get-tuple-element.17) | copy-start | bytes 6148
  712.4 105.2 %copy-start.2 = (s32[128,2]{0,1:T(2,128)S(1)}, s32[128,2]{0,1:T(2,128)}, u32[]{:S(2)}) copy-start(s32[128,2]{0,1:T(2,128)} %param.29) | copy-start | bytes 3076
  712.4 122.2 %copy-start.4 = (s32[256]{0:T(256)S(1)}, s32[256]{0:T(256)}, u32[]{:S(2)}) copy-start(s32[256]{0:T(256)} %copy-done.3) | copy-start | bytes 3076
  712.5 122.2 %copy-start.6 = (s32[256]{0:T(256)S(1)}, s32[256]{0:T(256)}, u32[]{:S(2)}) copy-start(s32[256]{0:T(256)} %copy-done.5) | copy-start | bytes 3076
  812.7 52.6 %all-to-all-start.5 = ((bf16[1,96,2,4096]{1,2,0,3:T(2,128)(2,1)}), bf16[1,96,2,4096]{1,2,0,3:T(2,128)(2,1)S(1)}, u32[]{:S(2)}, u32[]{:S(2)}) async-start(bf16[1,96,2,4096]{1,2,0,3:T(2,128)(2,1)} %copy.115), calls=%async_computation.6 | async-start | bytes 4194304 | tf_op jit(solution)/shard_map/all_to_all | solution.py:46
  871.8 6.3 copy-start.1
Sparse Core Ops, SparseCore 0:
  254.6 141.9 all-gather.1
  712.6 94.3 reduce-scatter.1
where the time goes:
time: 900 us; the launch traced here: 886 us
  local copies, waits for them, and re-layouts  352 us (39%)
  other arithmetic  236 us (26%)
  waiting for transfers between devices  162 us (18%)
  matrix products  62.3 us (7%)
  starting transfers between devices  28.7 us (3%)
  blocking collectives  27.7 us (3%)
  between operations  17.2 us (2%)
    unnamed x60, local copies, waits for them, and re-layouts  284 us
    unnamed x8, other arithmetic  218 us
    reduce_scatter x1, waiting for transfers between devices, mixture(): lax.psum_scatter(partial_terms, 'dp', scatter_dimension=0, tiled=True)  94.5 us
    all_to_all x1, waiting for transfers between devices, per_device(): lax.all_to_all(policy_gate, 'dp', split_axis=2, concat_axis=1, tiled=True)  36.7 us
    all_to_all x1, waiting for transfers between devices, mixture(): lax.all_to_all(summed.reshape(1, slot_count, models, model_width), 'exper...  30.7 us
    dot_general x2, matrix products, expert_terms(): jnp.dot(model_rows, up_weight, preferred_element_type=jnp.float32)  21.2 us
    dot_general x2, matrix products, expert_terms(): jnp.dot(model_rows, gate_weight, preferred_element_type=jnp.float32)  19.7 us
  transfers between devices with their start and end apart: 8, of which 3 were waited for; matrix products, arithmetic and copies ran while one was open for 62% of the time, Pallas kernels for 0%

commit v1 on v0

--- a/solution.py
+++ b/solution.py
@@ -18,15 +18,26 @@
     return (partial_logits, jnp.sum(values * values, axis=1))
 
 
-def expert_terms(piece_rows, weights):
+def expert_terms(slice_rows, weights):
     results = []
     for model_index in range(len(weights)):
         gate_weight, up_weight, down_weight = weights[model_index]
-        model_rows = piece_rows[:, model_index, :]
-        gate_value = jnp.dot(model_rows, gate_weight, preferred_element_type=jnp.float32)
-        up_value = jnp.dot(model_rows, up_weight, preferred_element_type=jnp.float32)
-        hidden = (jax.nn.silu(gate_value) * up_value).astype(jnp.bfloat16)
-        results.append(jnp.dot(hidden, down_weight, preferred_element_type=jnp.float32))
+        model_rows = slice_rows[:, model_index, :]
+        values = []
+        for weight in (gate_weight, up_weight):
+            partial = jnp.dot(model_rows, weight, preferred_element_type=jnp.float32)
+            values.append(
+                lax.psum_scatter(
+                    partial.astype(jnp.bfloat16), "dp", scatter_dimension=1, tiled=True
+                ).astype(jnp.float32)
+            )
+        hidden = (jax.nn.silu(values[0]) * values[1]).astype(jnp.bfloat16)
+        partial = jnp.dot(hidden, down_weight, preferred_element_type=jnp.float32)
+        results.append(
+            lax.psum_scatter(
+                partial.astype(jnp.bfloat16), "dp", scatter_dimension=0, tiled=True
+            )
+        )
     return jnp.stack(results, axis=1)
 
 
@@ -35,14 +46,8 @@
     model_width = expert_count * feature_block
     arrived_rows = lax.all_to_all(slot_rows, "expert", split_axis=0, concat_axis=3, tiled=True)
     local_rows = arrived_rows.reshape(slot_count, models, model_width)
-    partial_terms = expert_terms(
-        lax.all_gather(local_rows, "dp", axis=0, tiled=True), weights
-    ).astype(jnp.bfloat16)
-    summed = (
-        lax.psum_scatter(partial_terms, "dp", scatter_dimension=0, tiled=True)
-        .astype(jnp.float32)
-        .astype(jnp.bfloat16)
-    )
+    slice_rows = lax.all_to_all(local_rows, "dp", split_axis=2, concat_axis=0, tiled=True)
+    summed = expert_terms(slice_rows, weights)
     result = lax.all_to_all(
         summed.reshape(1, slot_count, models, model_width),
         "expert",
@@ -120,19 +125,13 @@
         mixed_rows = jnp.sum(picked * gates[:, :, None], axis=1) * live_mask[:, None]
         return mixed_rows.astype(jnp.bfloat16)
 
-    policy_gate_full, policy_up_full, reference_gate_full, reference_up_full = (
-        lax.all_to_all(policy_gate, "dp", split_axis=2, concat_axis=1, tiled=True),
-        lax.all_to_all(policy_up, "dp", split_axis=2, concat_axis=1, tiled=True),
-        lax.all_to_all(reference_gate, "dp", split_axis=2, concat_axis=1, tiled=True),
-        lax.all_to_all(reference_up, "dp", split_axis=2, concat_axis=1, tiled=True),
-    )
     stacked_rows = jnp.concatenate((policy_rows, reference_rows), axis=1)
     placed = jnp.dot(select, stacked_rows, preferred_element_type=jnp.float32).astype(jnp.bfloat16)
     expert_output = mixture(
         placed.reshape(expert_count, slot_count, 2, feature_block),
         (
-            (policy_gate_full[0], policy_up_full[0], policy_down[0]),
-            (reference_gate_full[0], reference_up_full[0], reference_down[0]),
+            (policy_gate[0], policy_up[0], policy_down[0]),
+            (reference_gate[0], reference_up[0], reference_down[0]),
         ),
     )
     policy_output = expert_output[:, :, 0, :]

time: 900 us -> 710 us (0.79); the launches traced: 886 us -> 709 us
  local copies, waits for them, and re-layouts: 352 us -> 25.6 us
  waiting for transfers between devices: 162 us -> 469 us
  other arithmetic: 236 us -> 13.9 us
  blocking collectives: 27.7 us -> 95.8 us
  starting transfers between devices: 28.7 us -> 5.01 us
  matrix products: 62.3 us -> 83.6 us
    reduce_scatter x1 -> x6, waiting for transfers between devices: 94.5 us -> 438 us  [the longest x4 321 us: expert_terms(): lax.psum_scatter(partial.astype(jnp.bfloat16), 'dp', scatter_dimension=1,...]
    unnamed x60 -> x9, local copies, waits for them, and re-layouts: 284 us -> 0.82 us
    unnamed x8 -> x1, other arithmetic: 218 us -> 0.07 us
    all_to_all x0 -> x2, blocking collectives: none -> 68.4 us  [the longest x1 38.3 us: mixture(): lax.all_to_all(slot_rows, 'expert', split_axis=0, concat_axis=3, tiled=True)]
    all_to_all x5 -> x1, local copies, waits for them, and re-layouts: 47 us -> 4.65 us  [mixture(): lax.all_to_all(local_rows, 'dp', split_axis=2, concat_axis=0, tiled=True)]
    all_to_all x5 -> x0, waiting for transfers between devices: 36.7 us -> none  [the longest x1 36.7 us: per_device(): lax.all_to_all(policy_gate, 'dp', split_axis=2, concat_axis=1, tiled=True)]
    all_to_all x5 -> x0, starting transfers between devices: 24 us -> none  [the longest x1 5.36 us: per_device(): lax.all_to_all(reference_up, 'dp', split_axis=2, concat_axis=1, tiled=True)]
    dot_general x6, matrix products: 58.8 us -> 80.1 us  [the longest x4 54.2 us: expert_terms(): partial = jnp.dot(model_rows, weight, preferred_element_type=jnp.float32)]
  transfers between devices with their start and end apart: 8 -> 7, of which waited for: 3 -> 7; matrix products, arithmetic and copies ran while one was open for 62% -> 10% of each run, Pallas kernels for 0% -> 0%
where the time goes in v1:
time: 710 us; the launch traced here: 709 us
  waiting for transfers between devices  469 us (66%)
  blocking collectives  95.8 us (13%)
  matrix products  83.6 us (12%)
  local copies, waits for them, and re-layouts  25.6 us (4%)
  between operations  16.8 us (2%)
  other arithmetic  13.9 us (2%)
    reduce_scatter x4, waiting for transfers between devices, expert_terms(): lax.psum_scatter(partial.astype(jnp.bfloat16), 'dp', scatter_dimension=1,...  321 us
    reduce_scatter x2, waiting for transfers between devices, expert_terms(): lax.psum_scatter(partial.astype(jnp.bfloat16), 'dp', scatter_dimension=0,...  117 us
    dot_general x4, matrix products, expert_terms(): partial = jnp.dot(model_rows, weight, preferred_element_type=jnp.float32)  54.2 us
    all_to_all x1, blocking collectives, mixture(): lax.all_to_all(slot_rows, 'expert', split_axis=0, concat_axis=3, tiled=True)  38.3 us
    all_to_all x1, waiting for transfers between devices, mixture(): lax.all_to_all(summed.reshape(1, slot_count, models, model_width), 'exper...  30.5 us
    all_to_all x1, blocking collectives, mixture(): lax.all_to_all(local_rows, 'dp', split_axis=2, concat_axis=0, tiled=True)  30.2 us
    dot_general x2, matrix products, expert_terms(): partial = jnp.dot(hidden, down_weight, preferred_element_type=jnp.float32)  25.9 us
  transfers between devices with their start and end apart: 7, of which 7 were waited for; matrix products, arithmetic and copies ran while one was open for 10% of the time, Pallas kernels for 0%

profile of v1, /device:TPU:0, one launch (start us, length us, event | category | flops | bytes accessed | tf_op | source)
XLA Modules:
  0.0 709.4 jit_solution(10029497235971331076)
XLA Ops:
  7.2 0.8 copy.85
  8.3 1.1 fusion.34
  9.4 1.1 fusion.35
  10.5 1.5 fusion.28
  11.9 1.5 fusion.30
  13.4 13.7 %all-reduce.1 = (f32[128]{0:T(128)S(1)}, f32[128]{0:T(128)S(1)}, f32[128,4]{0,1:T(4,128)S(1)}, f32[128,4]{0,1:T(4,128)S(1)}) all-reduce(f32[128]{0:T(128)S(1)} %fusion.35, f32[128]{0:T(128)S(1)} %fusion.34, f32[128,4]{0,1:T(4,128)S(1)} %fusion.30, f32[128,4]{0,1:T(4,128)S(1)} %fusion.28), channel_id=1, replica_groups=mesh['dp'=8,'expert'=4] {'expert'}, use_global_device_ids=true, to_apply=%region_7.8 | all-reduce | flops 1280 | bytes 10240 | tf_op jit(solution)/shard_map/psum | solution.py:86
  27.2 1.1 fusion.32
  28.2 1.1 fusion.33
  29.3 1.2 reduce-window.6
  31.1 0.7 multiply_add_fusion
  31.9 0.6 convolution_convert_fusion.4
  32.5 1.2 reshape.166
  33.7 0.4 copy.90
  34.1 38.3 %all_to_all.51 = bf16[4,96,2,1024]{3,1,2,0:T(8,128)(2,1)} all-to-all(bf16[4,96,2,1024]{3,1,2,0:T(8,128)(2,1)S(1)} %copy.90), channel_id=1, replica_groups=mesh['dp'=8,'expert'=4] {'expert'}, dimensions={0} | all-to-all | bytes 3145728 | tf_op jit(solution)/shard_map/all_to_all | solution.py:47
  72.4 4.6 copy.99
  77.0 30.2 %all_to_all.52 = bf16[96,2,4096]{0,1,2:T(2,128)(2,1)} all-to-all(bf16[96,2,4096]{0,1,2:T(2,128)(2,1)S(1)} %bitcast.74), channel_id=1, replica_groups=mesh['dp'=8,'expert'=4] {'dp'}, dimensions={2} | all-to-all | bytes 3145728 | tf_op jit(solution)/shard_map/all_to_all | solution.py:49
  107.2 4.7 copy.101
  111.9 13.0 %convolution_convert_fusion.3 = bf16[768,8192]{1,0:T(8,128)(2,1)} fusion(bf16[1,512,8192]{2,1,0:T(8,128)(2,1)} %param.23, bf16[768,2,512]{2,0,1:T(8,128)(2,1)S(1)} %bitcast.78), kind=kOutput, calls=%fused_computation.5 | convolution fusion | flops 6448742400 | bytes 21757952 | tf_op jit(solution)/shard_map/dot_general | solution.py:28
  124.9 15.1 %convolution_convert_fusion.2 = bf16[768,8192]{1,0:T(8,128)(2,1)} fusion(bf16[1,512,8192]{2,1,0:T(8,128)(2,1)} %param.24, bf16[768,2,512]{2,0,1:T(8,128)(2,1)S(1)} %bitcast.79), kind=kOutput, calls=%fused_computation.4 | convolution fusion | flops 6448742400 | bytes 21757952 | tf_op jit(solution)/shard_map/dot_general | solution.py:28
  140.0 0.2 reduce-scatter.13.cloned.1.call-start
  140.2 13.3 %convolution_convert_fusion.1 = bf16[768,8192]{1,0:T(8,128)(2,1)} fusion(bf16[1,512,8192]{2,1,0:T(8,128)(2,1)} %param.26, bf16[768,2,512]{2,0,1:T(8,128)(2,1)S(1)} %bitcast.80), kind=kOutput, calls=%fused_computation.3 | convolution fusion | flops 6448742400 | bytes 21757952 | tf_op jit(solution)/shard_map/dot_general | solution.py:28
  153.7 12.9 %convolution_convert_fusion = bf16[768,8192]{1,0:T(8,128)(2,1)} fusion(bf16[1,512,8192]{2,1,0:T(8,128)(2,1)} %param.27, bf16[768,2,512]{2,0,1:T(8,128)(2,1)S(1)} %bitcast.81), kind=kOutput, calls=%fused_computation.2 | convolution fusion | flops 6448742400 | bytes 21757952 | tf_op jit(solution)/shard_map/dot_general | solution.py:28
  166.6 47.6 %reduce-scatter.7.cloned.1.call-done = bf16[768,1024]{1,0:T(8,128)(2,1)} async-done(((bf16[768,8192]{1,0:T(8,128)(2,1)}), bf16[768,1024]{1,0:T(8,128)(2,1)}) %reduce-scatter.7.cloned.1.call-update) | async-done | bytes 1572880 | tf_op jit(solution)/shard_map/reduce_scatter | solution.py:30
  214.2 95.5 %reduce-scatter.9.cloned.1.call-done = bf16[768,1024]{1,0:T(8,128)(2,1)} async-done(((bf16[768,8192]{1,0:T(8,128)(2,1)}), bf16[768,1024]{1,0:T(8,128)(2,1)}) %reduce-scatter.9.cloned.1.call-update) | async-done | bytes 1572880 | tf_op jit(solution)/shard_map/reduce_scatter | solution.py:30
  309.7 13.1 %fusion.8 = bf16[768,4096]{1,0:T(8,128)(2,1)} fusion(bf16[1,1024,4096]{2,1,0:T(8,128)(2,1)} %param.25, bf16[768,1024]{1,0:T(8,128)(2,1)} %reduce-scatter.9.cloned.1.call-done, bf16[768,1024]{1,0:T(8,128)(2,1)} %reduce-scatter.7.cloned.1.call-done), kind=kOutput, calls=%fused_computation.14 | convolution fusion | flops 6451888128 | bytes 17825792 | tf_op jit(solution)/shard_map/dot_general | solution.py:35
  322.9 82.3 %reduce-scatter.13.cloned.1.call-done = bf16[768,1024]{1,0:T(8,128)(2,1)} async-done(((bf16[768,8192]{1,0:T(8,128)(2,1)}), bf16[768,1024]{1,0:T(8,128)(2,1)}) %reduce-scatter.13.cloned.1.call-update) | async-done | bytes 1572880 | tf_op jit(solution)/shard_map/reduce_scatter | solution.py:30
  405.3 95.4 %reduce-scatter.15.cloned.1.call-done = bf16[768,1024]{1,0:T(8,128)(2,1)} async-done(((bf16[768,8192]{1,0:T(8,128)(2,1)}), bf16[768,1024]{1,0:T(8,128)(2,1)}) %reduce-scatter.15.cloned.1.call-update) | async-done | bytes 1572880 | tf_op jit(solution)/shard_map/reduce_scatter | solution.py:30
  500.6 12.7 %fusion.11 = bf16[768,4096]{1,0:T(8,128)(2,1)} fusion(bf16[1,1024,4096]{2,1,0:T(8,128)(2,1)} %param.28, bf16[768,1024]{1,0:T(8,128)(2,1)} %reduce-scatter.15.cloned.1.call-done, bf16[768,1024]{1,0:T(8,128)(2,1)} %reduce-scatter.13.cloned.1.call-done), kind=kOutput, calls=%fused_computation.15 | convolution fusion | flops 6451888128 | bytes 17825792 | tf_op jit(solution)/shard_map/dot_general | solution.py:35
  513.4 52.2 %reduce-scatter.11.cloned.1.call-done = bf16[96,4096]{1,0:T(8,128)(2,1)} async-done(((bf16[768,4096]{1,0:T(8,128)(2,1)}), bf16[96,4096]{1,0:T(8,128)(2,1)}) %reduce-scatter.11.cloned.1.call-update) | async-done | bytes 786448 | tf_op jit(solution)/shard_map/reduce_scatter | solution.py:37
  565.6 65.0 %reduce-scatter.17.cloned.1.call-done = bf16[96,4096]{1,0:T(8,128)(2,1)} async-done(((bf16[768,4096]{1,0:T(8,128)(2,1)}), bf16[96,4096]{1,0:T(8,128)(2,1)}) %reduce-scatter.17.cloned.1.call-update) | async-done | bytes 786448 | tf_op jit(solution)/shard_map/reduce_scatter | solution.py:37
  630.6 1.5 maximum_bitcast_fusion
  632.2 4.0 copy.95
  636.1 4.6 all-to-all-start.2
  641.0 0.2 multiply_reduce_fusion.2
  641.2 1.1 fusion.54
  642.3 13.7 %all-reduce = (f32[]{:T(128)}, f32[4]{0:T(128)S(1)}, f32[4]{0:T(128)S(1)}) all-reduce(f32[]{:T(128)} %get-tuple-element.18, f32[4]{0:T(128)S(1)} %get-tuple-element.6, f32[4]{0:T(128)S(1)} %get-tuple-element.10), channel_id=1, replica_groups=mesh['dp'=8,'expert'=4] {'dp'}, use_global_device_ids=true, to_apply=%region_28.31 | all-reduce | flops 9 | bytes 72 | tf_op jit(solution)/shard_map/psum | solution.py:148
  656.3 0.6 multiply_reduce_fusion.4
  658.3 30.5 %all-to-all-done.2 = bf16[1,96,2,4096]{1,2,0,3:T(2,128)(2,1)S(1)} async-done(((bf16[1,96,2,4096]{1,2,0,3:T(2,128)(2,1)}), bf16[1,96,2,4096]{1,2,0,3:T(2,128)(2,1)S(1)}, u32[]{:S(2)}, u32[]{:S(2)}) %all-to-all-start.2) | async-done | bytes 1572896 | tf_op jit(solution)/shard_map/all_to_all | solution.py:51
  688.7 3.7 copy.96
  692.4 1.6 fusion.57
  694.0 1.2 gather_fusion
  695.2 1.2 gather_fusion.1
  696.3 0.2 select_convert_fusion
  696.6 0.6 reshape.169
  697.2 0.6 reshape.170
  697.8 1.3 multiply_reduce_fusion.1
  699.2 1.3 multiply_reduce_fusion
  700.5 0.9 multiply_convert_fusion
  (54 shorter events, 1.9 us)
Async XLA Ops:
  7.2 3.3 copy-start
  7.2 207.0 %reduce-scatter.7.cloned.1.call-start = ((), (), s32[]{:S(2)}) async-start(), calls=%async_computation.9 | async-start | bytes 14155776 | tf_op jit(solution)/shard_map/reduce_scatter | solution.py:30
  124.9 184.9 %reduce-scatter.9.cloned.1.call-start = ((), (), s32[]{:S(2)}) async-start(), calls=%async_computation.10 | async-start | bytes 14155776 | tf_op jit(solution)/shard_map/reduce_scatter | solution.py:30
  140.0 265.2 %reduce-scatter.13.cloned.1.call-start = ((), (), s32[]{:S(2)}) async-start(), calls=%async_computation.12 | async-start | bytes 14155776 | tf_op jit(solution)/shard_map/reduce_scatter | solution.py:30
  153.6 347.0 %reduce-scatter.15.cloned.1.call-start = ((), (), s32[]{:S(2)}) async-start(), calls=%async_computation.13 | async-start | bytes 14155776 | tf_op jit(solution)/shard_map/reduce_scatter | solution.py:30
  166.5 399.1 %reduce-scatter.11.cloned.1.call-start = ((), (), s32[]{:S(2)}) async-start(), calls=%async_computation.11 | async-start | bytes 7077888 | tf_op jit(solution)/shard_map/reduce_scatter | solution.py:37
  322.9 307.7 %reduce-scatter.17.cloned.1.call-start = ((), (), s32[]{:S(2)}) async-start(), calls=%async_computation.14 | async-start | bytes 7077888 | tf_op jit(solution)/shard_map/reduce_scatter | solution.py:37
  632.1 8.6 %copy-start.3 = (s32[4]{0:T(128)S(1)}, s32[4]{0:T(128)}, u32[]{:S(2)}) copy-start(s32[4]{0:T(128)} %param.30) | copy-start | bytes 52
  632.1 8.8 %copy-start.2 = (s32[128,2]{0,1:T(2,128)S(1)}, s32[128,2]{0,1:T(2,128)}, u32[]{:S(2)}) copy-start(s32[128,2]{0,1:T(2,128)} %param.29) | copy-start | bytes 3076
  636.1 52.6 %all-to-all-start.2 = ((bf16[1,96,2,4096]{1,2,0,3:T(2,128)(2,1)}), bf16[1,96,2,4096]{1,2,0,3:T(2,128)(2,1)S(1)}, u32[]{:S(2)}, u32[]{:S(2)}) async-start(bf16[1,96,2,4096]{1,2,0,3:T(2,128)(2,1)} %copy.95), calls=%async_computation.8 | async-start | bytes 4194304 | tf_op jit(solution)/shard_map/all_to_all | solution.py:51
  697.2 4.3 copy-start.1
Sparse Core Ops, SparseCore 0:
  125.0 89.1 reduce-scatter.6
  217.7 91.9 reduce-scatter.8
  313.2 91.9 reduce-scatter.12
  408.6 91.9 reduce-scatter.14
  503.8 61.7 reduce-scatter.10
  568.8 61.7 reduce-scatter.16
